TPU v7x, 32 devices: a whole 2x2x4 slice. The times are simulated.
32 devices in a mesh: lon: 8 (over y, x, core), lat: 4 (over z).
Axes of the slice: x: 2, y: 2, z: 4, core: 2. Of those that a mesh axis runs over, the one named last changes fastest.
Arguments:
- fields: bfloat16 [4, 128, 32, 1024], P(None, None, 'lat', 'lon'), may hold values from -12 to 12
- bracket: int32 [32, 32, 1024], P(None, 'lat', 'lon'), may hold values from 0 to 126, as said below
- fraction: bfloat16 [32, 32, 1024], P(None, 'lat', 'lon'), may hold values from 0 to 1
Outputs:
- on_pressure: bfloat16 [4, 32, 32, 1024], P(None, None, ('lat', 'lon'))
- zonal_mean: float32 [4, 32, 32], P(None, None, ('lat', 'lon'))
- meridional: float32 [4, 32, 32], P(None, None, ('lat', 'lon'))
Inputs may be any that keep to these rules, and one draw needn't show every extreme that they name: bracket[p, r, c] - min(p * 4, 112) lies in 0 to 14 for every column, and each of these offsets occurs.
All inputs are finite; a program needn't handle non-finite values.
Results may differ from a plain program's by a relative error of at most 0.0012.
Values may be sent and summed in bfloat16 or wider, within the bound.
A program may use at most 128 MiB of HBM per device.

v0:
```python
import functools

import jax
import jax.numpy as jnp
from jax import lax
from jax.experimental import pallas as pl
from jax.experimental.pallas import tpu as pltpu
from jax.sharding import PartitionSpec as P

WINDOW = 16
TILE = 8
MESH = pl.DeviceIdType.MESH


def select_pair(levels, masks):
    bit = len(levels) // 2
    for mask in masks:
        levels = [
            jnp.where(mask, levels[k + bit], levels[k]) if k + bit < len(levels) else levels[k]
            for k in range(bit + 1)
        ]
        bit //= 2
    return levels


def kernel(
    lon_count, lat_count, fields_hbm, bracket_hbm, fraction_hbm,
    out_ref, zonal_ref, merid_ref,
    fields, bracket, fraction, send, sums, cross_lo, cross_hi,
    in_sem, field_sem, own_sem, send_sem, recv_sem, sum_send, sum_recv,
    cross_send, lo_recv, hi_recv,
):
    var_count, level_count, row_count, lons = fields.shape
    plev_count = bracket.shape[0]
    own = row_count // lon_count
    group_size = min(TILE, plev_count)
    level_step = level_count // plev_count
    me = lax.axis_index("lon")
    band = lax.axis_index("lat")
    next_band = (band + 1) % lat_count
    prev_band = (band + lat_count - 1) % lat_count
    has_lo = jnp.logical_and(me == 0, band > 0)
    has_hi = jnp.logical_and(me == lon_count - 1, band < lat_count - 1)
    my_lons = pl.ds(pl.multiple_of(me * lons, 128), lons)

    get_bracket = pltpu.make_async_copy(bracket_hbm, bracket, in_sem.at[0])
    get_fraction = pltpu.make_async_copy(fraction_hbm, fraction, in_sem.at[1])

    def get_fields(v):
        return pltpu.make_async_copy(fields_hbm.at[v], fields.at[v], field_sem.at[v])

    get_bracket.start()
    get_fraction.start()
    for v in range(var_count):
        get_fields(v).start()

    barrier = pltpu.get_barrier_semaphore()
    for step in range(1, lon_count):
        peer = (me + step) % lon_count
        pl.semaphore_signal(barrier, inc=1, device_id={"lon": peer}, device_id_type=MESH)

    @pl.when(has_lo)
    def _():
        for l in range(lon_count):
            pl.semaphore_signal(barrier, inc=1, device_id={"lon": l, "lat": prev_band}, device_id_type=MESH)

    @pl.when(has_hi)
    def _():
        for l in range(lon_count):
            pl.semaphore_signal(barrier, inc=1, device_id={"lon": l, "lat": next_band}, device_id_type=MESH)

    def block_copy(v, step):
        peer = (me + step) % lon_count
        return pltpu.make_async_remote_copy(
            src_ref=send.at[v, pl.ds(peer * own, own)],
            dst_ref=out_ref.at[v, :, :, my_lons],
            send_sem=send_sem.at[step],
            recv_sem=recv_sem.at[step],
            device_id={"lon": peer},
            device_id_type=MESH,
        )

    def own_copy(v):
        return pltpu.make_async_copy(
            send.at[v, pl.ds(me * own, own)], out_ref.at[v, :, :, my_lons], own_sem.at[v]
        )

    def sum_copy(step):
        return pltpu.make_async_remote_copy(
            src_ref=sums.at[me],
            dst_ref=sums.at[me],
            send_sem=sum_send.at[step],
            recv_sem=sum_recv.at[step],
            device_id={"lon": (me + step) % lon_count},
            device_id_type=MESH,
        )

    def up_copy():
        return pltpu.make_async_remote_copy(
            src_ref=sums.at[me], dst_ref=cross_lo.at[me],
            send_sem=cross_send.at[0], recv_sem=lo_recv.at[me],
            device_id={"lon": 0, "lat": next_band}, device_id_type=MESH,
        )

    def down_copy():
        return pltpu.make_async_remote_copy(
            src_ref=sums.at[me], dst_ref=cross_hi.at[me],
            send_sem=cross_send.at[1], recv_sem=hi_recv.at[me],
            device_id={"lon": lon_count - 1, "lat": prev_band}, device_id_type=MESH,
        )

    get_bracket.wait()
    get_fraction.wait()
    ones = jnp.ones((TILE, lons), jnp.bfloat16)

    @pl.loop(0, var_count)
    def _(v):
        get_fields(v).wait()

        @pl.loop(0, row_count // TILE)
        def _(tile):
            rows = pl.ds(pl.multiple_of(tile * TILE, TILE), TILE)
            loaded, group = {}, []
            for p in range(plev_count):
                base = min(p * level_step, level_count - WINDOW)
                for k in range(base, base + WINDOW):
                    if k not in loaded:
                        loaded[k] = fields[v, k, rows, :].astype(jnp.float32)
                offset = bracket[p, rows, :] - base
                masks, bit = [], WINDOW // 2
                while bit:
                    masks.append((offset & bit) != 0)
                    bit //= 2
                lower, upper = select_pair([loaded[base + k] for k in range(WINDOW)], masks)
                weight = fraction[p, rows, :].astype(jnp.float32)
                group.append(lower + weight * (upper - lower))
                if len(group) == group_size:
                    by_row = jnp.transpose(jnp.stack(group), (1, 0, 2)).astype(jnp.bfloat16)
                    send[v, rows, p + 1 - group_size : p + 1, :] = by_row
                    group = []
            rounded = send[v, rows].reshape(TILE * plev_count, lons)
            total = lax.dot_general(
                ones, rounded, (((1,), (1,)), ((), ())), preferred_element_type=jnp.float32
            )
            width = TILE * plev_count
            sums[me, v, :, pl.ds(pl.multiple_of(tile * width, width), width)] = total[0:1]

        @pl.when(v == 0)
        def _():
            beyond = (band < lat_count - 1).astype(jnp.int32) + (band > 0).astype(jnp.int32)
            pl.semaphore_wait(barrier, lon_count - 1 + beyond)

        for step in range(lon_count - 1, 0, -1):
            block_copy(v, step).start()
        own_copy(v).start()

    @pl.when(band < lat_count - 1)
    def _():
        up_copy().start()

    @pl.when(band > 0)
    def _():
        down_copy().start()

    for step in range(1, lon_count):
        sum_copy(step).start()

    for step in range(1, lon_count):
        sum_copy(step).wait_recv()
    mean = sums[0]
    for l in range(1, lon_count):
        mean = mean + sums[l]
    count = jnp.float32(lons * lon_count)
    mean = mean / count
    width = row_count * plev_count

    def row_of(q):
        shift = (2 * width - q * plev_count) % width
        return pltpu.roll(mean.reshape(var_count, width), shift, 1)[:, :plev_count]

    def edge(cross, recv, row):
        for l in range(lon_count):
            pltpu.make_async_copy(cross.at[l], cross.at[l], recv.at[l]).wait()
        total = cross[0]
        for l in range(1, lon_count):
            total = total + cross[l]
        total = (total / count).reshape(var_count, width)
        return total[:, row * plev_count : (row + 1) * plev_count]

    first = me * own
    for j in range(own):
        here = row_of(first + j)
        below = row_of(first + j - 1)
        above = row_of(first + j + 1)
        zonal_ref[:, j, :] = here
        lower_edge = jnp.logical_and(first + j == 0, band == 0)
        upper_edge = jnp.logical_and(first + j == row_count - 1, band == lat_count - 1)
        below = jnp.where(lower_edge, here, below)
        above = jnp.where(upper_edge, here, above)
        scale = jnp.where(jnp.logical_or(lower_edge, upper_edge), 1.0, 0.5)
        merid_ref[:, j, :] = scale * (above - below)

    @pl.when(has_lo)
    def _():
        below = edge(cross_lo, lo_recv, row_count - 1)
        above = row_of(jnp.int32(1))
        merid_ref[:, 0, :] = 0.5 * (above - below)

    @pl.when(has_hi)
    def _():
        above = edge(cross_hi, hi_recv, 0)
        below = row_of(jnp.int32(row_count - 2))
        merid_ref[:, own - 1, :] = 0.5 * (above - below)

    for v in range(var_count):
        own_copy(v).wait()
    for step in range(1, lon_count):
        source = (me + lon_count - step) % lon_count
        landed = out_ref.at[:, :, :, pl.ds(pl.multiple_of(source * lons, 128), lons)]
        pltpu.make_async_copy(landed, landed, recv_sem.at[step]).wait()
    for step in range(1, lon_count):
        peer = (me + step) % lon_count
        left = send.at[:, pl.ds(peer * own, own)]
        pltpu.make_async_copy(left, left, send_sem.at[step]).wait()
        sum_copy(step).wait_send()

    @pl.when(band < lat_count - 1)
    def _():
        up_copy().wait_send()

    @pl.when(band > 0)
    def _():
        down_copy().wait_send()


def shards(lon_count, lat_count, fields, bracket, fraction):
    var_count, level_count, row_count, lons = fields.shape
    plev_count = bracket.shape[0]
    own = row_count // lon_count
    sum_shape = (lon_count, var_count, 1, row_count * plev_count)
    dma = pltpu.SemaphoreType.DMA
    anywhere = pl.BlockSpec(memory_space=pl.ANY)
    in_vmem = pl.BlockSpec(memory_space=pltpu.VMEM)
    on_pressure, zonal_mean, meridional = pl.pallas_call(
        functools.partial(kernel, lon_count, lat_count),
        out_shape=(
            jax.ShapeDtypeStruct((var_count, own, plev_count, lons * lon_count), jnp.bfloat16),
            jax.ShapeDtypeStruct((var_count, own, plev_count), jnp.float32),
            jax.ShapeDtypeStruct((var_count, own, plev_count), jnp.float32),
        ),
        in_specs=[anywhere] * 3,
        out_specs=(anywhere, in_vmem, in_vmem),
        scratch_shapes=[
            pltpu.VMEM(fields.shape, fields.dtype),
            pltpu.VMEM(bracket.shape, bracket.dtype),
            pltpu.VMEM(fraction.shape, fraction.dtype),
            pltpu.VMEM((var_count, row_count, plev_count, lons), jnp.bfloat16),
            pltpu.VMEM(sum_shape, jnp.float32),
            pltpu.VMEM(sum_shape, jnp.float32),
            pltpu.VMEM(sum_shape, jnp.float32),
            dma((2,)),
            dma((var_count,)),
            dma((var_count,)),
            dma((lon_count,)),
            dma((lon_count,)),
            dma((lon_count,)),
            dma((lon_count,)),
            dma((2,)),
            dma((lon_count,)),
            dma((lon_count,)),
        ],
        compiler_params=pltpu.CompilerParams(
            collective_id=0, has_side_effects=True, vmem_limit_bytes=60 * 1024 * 1024
        ),
    )(fields, bracket, fraction)
    return (
        on_pressure.transpose(0, 2, 1, 3),
        zonal_mean.transpose(0, 2, 1),
        meridional.transpose(0, 2, 1),
    )


def solution(mesh):
    return jax.shard_map(
        functools.partial(shards, mesh.shape["lon"], mesh.shape["lat"]),
        mesh=mesh,
        in_specs=(P(None, None, "lat", "lon"), P(None, "lat", "lon"), P(None, "lat", "lon")),
        out_specs=(
            P(None, None, ("lat", "lon"), None),
            P(None, None, ("lat", "lon")),
            P(None, None, ("lat", "lon")),
        ),
        check_vma=False,
    )
```

profile of v0, /device:TPU:0, one launch (start us, length us, event | category | flops | bytes accessed | tf_op | source)
XLA Modules:
  0.0 14.5 jit_solution(9978119906809387487)
XLA Ops:
  0.6 10.9 %shard_map.58 = (bf16[4,1,32,1024]{3,2,1,0:T(8,128)(2,1)}, f32[4,1,32]{2,1,0:T(1,128)}, f32[4,1,32]{2,1,0:T(1,128)}) custom-call(bf16[4,128,8,128]{3,2,1,0:T(8,128)(2,1)} %fields_hbm.1, s32[32,8,128]{2,1,0:T(8,128)} %bracket_hbm.1, bf16[32,8,128]{2,1,0:T(8,128)(2,1)} %fraction_hbm.1), custom_call_target="tpu_custom_call" | custom-call | tf_op jit(solution)/shard_map/pallas_call | solution.py:244
  11.6 0.0 copy-start.1
  11.6 1.7 %copy.12 = bf16[4,32,1,1024]{3,1,2,0:T(8,128)(2,1)} copy(bf16[4,32,1,1024]{3,1,2,0:T(8,128)(2,1)} %bitcast.9) | data formatting | bytes 524288
  13.2 0.0 copy-done.1
  13.2 0.0 copy-start
  13.2 0.6 %copy.13 = f32[4,32,1]{1,2,0:T(1,128)} copy(f32[4,32,1]{1,2,0:T(1,128)S(1)} %bitcast.11) | data formatting | bytes 1024
  13.8 0.1 copy-done
  13.9 0.6 %copy.14 = f32[4,32,1]{1,2,0:T(1,128)} copy(f32[4,32,1]{1,2,0:T(1,128)S(1)} %bitcast.10) | data formatting | bytes 1024
Async XLA Ops:
  11.6 1.7 %copy-start.1 = (f32[4,1,32]{2,1,0:T(1,128)S(1)}, f32[4,1,32]{2,1,0:T(1,128)}, u32[]{:S(2)}) copy-start(f32[4,1,32]{2,1,0:T(1,128)} %get-tuple-element.7) | copy-start | bytes 1540
  13.2 0.7 %copy-start = (f32[4,1,32]{2,1,0:T(1,128)S(1)}, f32[4,1,32]{2,1,0:T(1,128)}, u32[]{:S(2)}) copy-start(f32[4,1,32]{2,1,0:T(1,128)} %get-tuple-element.8) | copy-start | bytes 1540
where the time goes:
time: 14.7 us; the launch traced here: 14.5 us
  Pallas kernels  10.9 us (74%)
  local copies, waits for them, and re-layouts  2.93 us (20%)
  between operations  0.65 us (4%)
    pallas_call x1, Pallas kernels, shards(): pl.pallas_call(functools.partial(kernel, lon_count, lat_count), out_shape...  10.9 us
    unnamed x7, local copies, waits for them, and re-layouts  2.93 us

commit v1 on v0

--- a/solution.py
+++ b/solution.py
@@ -23,10 +23,10 @@
     return levels
 
 
-def kernel(
+def exchange(
     lon_count, lat_count, fields_hbm, bracket_hbm, fraction_hbm,
-    out_ref, zonal_ref, merid_ref,
-    fields, bracket, fraction, send, sums, cross_lo, cross_hi,
+    out_ref, sums, cross_lo, cross_hi,
+    fields, bracket, fraction, send,
     in_sem, field_sem, own_sem, send_sem, recv_sem, sum_send, sum_recv,
     cross_send, lo_recv, hi_recv,
 ):
@@ -167,10 +167,54 @@
 
     for step in range(1, lon_count):
         sum_copy(step).wait_recv()
+
+    @pl.when(has_lo)
+    def _():
+        for l in range(lon_count):
+            pltpu.make_async_copy(cross_lo.at[l], cross_lo.at[l], lo_recv.at[l]).wait()
+
+    @pl.when(has_hi)
+    def _():
+        for l in range(lon_count):
+            pltpu.make_async_copy(cross_hi.at[l], cross_hi.at[l], hi_recv.at[l]).wait()
+
+    for v in range(var_count):
+        own_copy(v).wait()
+    for step in range(1, lon_count):
+        source = (me + lon_count - step) % lon_count
+        landed = out_ref.at[:, :, :, pl.ds(pl.multiple_of(source * lons, 128), lons)]
+        pltpu.make_async_copy(landed, landed, recv_sem.at[step]).wait()
+    for step in range(1, lon_count):
+        peer = (me + step) % lon_count
+        left = send.at[:, pl.ds(peer * own, own)]
+        pltpu.make_async_copy(left, left, send_sem.at[step]).wait()
+        sum_copy(step).wait_send()
+
+    @pl.when(band < lat_count - 1)
+    def _():
+        up_copy().wait_send()
+
+    @pl.when(band > 0)
+    def _():
+        down_copy().wait_send()
+
+
+def finish(
+    lon_count, lat_count, count, rows_vmem, sums, cross_lo, cross_hi,
+    out_hbm, zonal_hbm, merid_hbm, zonal, merid, sem,
+):
+    var_count, own, plev_count = zonal.shape
+    row_count = own * lon_count
+    me = lax.axis_index("lon")
+    band = lax.axis_index("lat")
+    has_lo = jnp.logical_and(me == 0, band > 0)
+    has_hi = jnp.logical_and(me == lon_count - 1, band < lat_count - 1)
+    put_rows = pltpu.make_async_copy(rows_vmem, out_hbm, sem.at[0])
+    put_rows.start()
+
     mean = sums[0]
     for l in range(1, lon_count):
         mean = mean + sums[l]
-    count = jnp.float32(lons * lon_count)
     mean = mean / count
     width = row_count * plev_count
 
@@ -178,9 +222,7 @@
         shift = (2 * width - q * plev_count) % width
         return pltpu.roll(mean.reshape(var_count, width), shift, 1)[:, :plev_count]
 
-    def edge(cross, recv, row):
-        for l in range(lon_count):
-            pltpu.make_async_copy(cross.at[l], cross.at[l], recv.at[l]).wait()
+    def edge(cross, row):
         total = cross[0]
         for l in range(1, lon_count):
             total = total + cross[l]
@@ -192,45 +234,33 @@
         here = row_of(first + j)
         below = row_of(first + j - 1)
         above = row_of(first + j + 1)
-        zonal_ref[:, j, :] = here
+        zonal[:, j, :] = here
         lower_edge = jnp.logical_and(first + j == 0, band == 0)
         upper_edge = jnp.logical_and(first + j == row_count - 1, band == lat_count - 1)
         below = jnp.where(lower_edge, here, below)
         above = jnp.where(upper_edge, here, above)
         scale = jnp.where(jnp.logical_or(lower_edge, upper_edge), 1.0, 0.5)
-        merid_ref[:, j, :] = scale * (above - below)
+        merid[:, j, :] = scale * (above - below)
 
     @pl.when(has_lo)
     def _():
-        below = edge(cross_lo, lo_recv, row_count - 1)
+        below = edge(cross_lo, row_count - 1)
         above = row_of(jnp.int32(1))
-        merid_ref[:, 0, :] = 0.5 * (above - below)
+        merid[:, 0, :] = 0.5 * (above - below)
 
     @pl.when(has_hi)
     def _():
-        above = edge(cross_hi, hi_recv, 0)
+        above = edge(cross_hi, 0)
         below = row_of(jnp.int32(row_count - 2))
-        merid_ref[:, own - 1, :] = 0.5 * (above - below)
-
-    for v in range(var_count):
-        own_copy(v).wait()
-    for step in range(1, lon_count):
-        source = (me + lon_count - step) % lon_count
-        landed = out_ref.at[:, :, :, pl.ds(pl.multiple_of(source * lons, 128), lons)]
-        pltpu.make_async_copy(landed, landed, recv_sem.at[step]).wait()
-    for step in range(1, lon_count):
-        peer = (me + step) % lon_count
-        left = send.at[:, pl.ds(peer * own, own)]
-        pltpu.make_async_copy(left, left, send_sem.at[step]).wait()
-        sum_copy(step).wait_send()
-
-    @pl.when(band < lat_count - 1)
-    def _():
-        up_copy().wait_send()
-
-    @pl.when(band > 0)
-    def _():
-        down_copy().wait_send()
+        merid[:, own - 1, :] = 0.5 * (above - below)
+
+    put_zonal = pltpu.make_async_copy(zonal, zonal_hbm, sem.at[1])
+    put_merid = pltpu.make_async_copy(merid, merid_hbm, sem.at[2])
+    put_zonal.start()
+    put_merid.start()
+    put_rows.wait()
+    put_zonal.wait()
+    put_merid.wait()
 
 
 def shards(lon_count, lat_count, fields, bracket, fraction):
@@ -240,24 +270,25 @@
     sum_shape = (lon_count, var_count, 1, row_count * plev_count)
     dma = pltpu.SemaphoreType.DMA
     anywhere = pl.BlockSpec(memory_space=pl.ANY)
+    room = 2 * fields.size + 4 * bracket.size + 2 * fraction.size * (1 + var_count)
     in_vmem = pl.BlockSpec(memory_space=pltpu.VMEM)
-    on_pressure, zonal_mean, meridional = pl.pallas_call(
-        functools.partial(kernel, lon_count, lat_count),
+    rows_shape = (var_count, own, plev_count, lons * lon_count)
+    inputs = [pltpu.with_memory_space_constraint(x, pltpu.HBM) for x in (fields, bracket, fraction)]
+    held = pl.pallas_call(
+        functools.partial(exchange, lon_count, lat_count),
         out_shape=(
-            jax.ShapeDtypeStruct((var_count, own, plev_count, lons * lon_count), jnp.bfloat16),
-            jax.ShapeDtypeStruct((var_count, own, plev_count), jnp.float32),
-            jax.ShapeDtypeStruct((var_count, own, plev_count), jnp.float32),
+            pltpu.VMEM(rows_shape, jnp.bfloat16),
+            pltpu.VMEM(sum_shape, jnp.float32),
+            pltpu.VMEM(sum_shape, jnp.float32),
+            pltpu.VMEM(sum_shape, jnp.float32),
         ),
         in_specs=[anywhere] * 3,
-        out_specs=(anywhere, in_vmem, in_vmem),
+        out_specs=(in_vmem,) * 4,
         scratch_shapes=[
             pltpu.VMEM(fields.shape, fields.dtype),
             pltpu.VMEM(bracket.shape, bracket.dtype),
             pltpu.VMEM(fraction.shape, fraction.dtype),
             pltpu.VMEM((var_count, row_count, plev_count, lons), jnp.bfloat16),
-            pltpu.VMEM(sum_shape, jnp.float32),
-            pltpu.VMEM(sum_shape, jnp.float32),
-            pltpu.VMEM(sum_shape, jnp.float32),
             dma((2,)),
             dma((var_count,)),
             dma((var_count,)),
@@ -270,9 +301,27 @@
             dma((lon_count,)),
         ],
         compiler_params=pltpu.CompilerParams(
-            collective_id=0, has_side_effects=True, vmem_limit_bytes=60 * 1024 * 1024
+            collective_id=0, has_side_effects=True, vmem_limit_bytes=room + (8 << 20)
         ),
-    )(fields, bracket, fraction)
+    )(*inputs)
+    held = [pltpu.with_memory_space_constraint(x, pltpu.VMEM) for x in held]
+    mean_shape = (var_count, own, plev_count)
+    on_pressure, zonal_mean, meridional = pl.pallas_call(
+        functools.partial(finish, lon_count, lat_count, float(lons * lon_count)),
+        out_shape=(
+            jax.ShapeDtypeStruct(rows_shape, jnp.bfloat16),
+            jax.ShapeDtypeStruct(mean_shape, jnp.float32),
+            jax.ShapeDtypeStruct(mean_shape, jnp.float32),
+        ),
+        in_specs=[in_vmem] * 4,
+        out_specs=(anywhere,) * 3,
+        scratch_shapes=[
+            pltpu.VMEM(mean_shape, jnp.float32),
+            pltpu.VMEM(mean_shape, jnp.float32),
+            dma((3,)),
+        ],
+        compiler_params=pltpu.CompilerParams(vmem_limit_bytes=8 << 20),
+    )(*held)
     return (
         on_pressure.transpose(0, 2, 1, 3),
         zonal_mean.transpose(0, 2, 1),

time: 14.7 us -> 11.7 us (0.80)
  local copies, waits for them, and re-layouts: 2.93 us -> 0 us
    unnamed x7 -> x0, local copies, waits for them, and re-layouts: 2.93 us -> none
    pallas_call x1 -> x2, Pallas kernels: 10.9 us -> 10.9 us  [the longest x1 10.2 us: shards(): pl.pallas_call(functools.partial(exchange, lon_count, lat_count), out_sha...]
where the time goes in v1:
time: 11.7 us; the launch traced here: 11.6 us
  Pallas kernels  10.9 us (93%)
  between operations  0.64 us (5%)
    pallas_call x1, Pallas kernels, shards(): pl.pallas_call(functools.partial(exchange, lon_count, lat_count), out_sha...  10.2 us
    pallas_call x1, Pallas kernels, shards(): pl.pallas_call(functools.partial(finish, lon_count, lat_count, float(lons...  0.76 us

profile of v1, /device:TPU:0, one launch (start us, length us, event | category | flops | bytes accessed | tf_op | source)
XLA Modules:
  0.0 11.6 jit_solution(16311650409287398779)
XLA Ops:
  0.6 10.2 %shard_map.58 = (bf16[4,1,32,1024]{3,2,1,0:T(8,128)(2,1)S(1)}, f32[8,4,1,256]{3,2,1,0:T(1,128)S(1)}, f32[8,4,1,256]{3,2,1,0:T(1,128)S(1)}, f32[8,4,1,256]{3,2,1,0:T(1,128)S(1)}) custom-call(bf16[4,128,8,128]{3,2,1,0:T(8,128)(2,1)} %fields_hbm.1, s32[32,8,128]{2,1,0:T(8,128)} %bracket_hbm.1, bf16[32,8,128]{2,1,0:T(8,128)(2,1)} %fraction_hbm.1), custom_call_target="tpu_custom_call" | custom-call | tf_op jit(solution)/shard_map/pallas_call | solution.py:277
  10.8 0.8 %shard_map.59 = (bf16[4,1,32,1024]{3,2,1,0:T(8,128)(2,1)}, f32[4,1,32]{2,1,0:T(1,128)}, f32[4,1,32]{2,1,0:T(1,128)}) custom-call(bf16[4,1,32,1024]{3,2,1,0:T(8,128)(2,1)S(1)} %get-tuple-element.10.rows_vmem, f32[8,4,1,256]{3,2,1,0:T(1,128)S(1)} %get-tuple-element.11.sums, f32[8,4,1,256]{3,2,1,0:T(1,128)S(1)} %get-tuple-element.12.cross_lo, ...), custom_call_target="tpu_custom_call" | custom-call | tf_op jit(solution)/shard_map/pallas_call | solution.py:309

commit v2 on v1

--- a/solution.py
+++ b/solution.py
@@ -150,20 +150,22 @@
             beyond = (band < lat_count - 1).astype(jnp.int32) + (band > 0).astype(jnp.int32)
             pl.semaphore_wait(barrier, lon_count - 1 + beyond)
 
+        @pl.when(v == var_count - 1)
+        def _():
+            @pl.when(band < lat_count - 1)
+            def _():
+                up_copy().start()
+
+            @pl.when(band > 0)
+            def _():
+                down_copy().start()
+
+            for step in range(1, lon_count):
+                sum_copy(step).start()
+
         for step in range(lon_count - 1, 0, -1):
             block_copy(v, step).start()
         own_copy(v).start()
-
-    @pl.when(band < lat_count - 1)
-    def _():
-        up_copy().start()
-
-    @pl.when(band > 0)
-    def _():
-        down_copy().start()
-
-    for step in range(1, lon_count):
-        sum_copy(step).start()
 
     for step in range(1, lon_count):
         sum_copy(step).wait_recv()

time: 11.7 us -> 11.8 us (level)
  no operation moved by 1% of the time
where the time goes in v2:
time: 11.8 us; the launch traced here: 11.7 us
  Pallas kernels  11 us (93%)
  between operations  0.64 us (5%)
    pallas_call x1, Pallas kernels, shards(): pl.pallas_call(functools.partial(exchange, lon_count, lat_count), out_sha...  10.3 us
    pallas_call x1, Pallas kernels, shards(): pl.pallas_call(functools.partial(finish, lon_count, lat_count, float(lons...  0.76 us

profile of v2, /device:TPU:0, one launch (start us, length us, event | category | flops | bytes accessed | tf_op | source)
XLA Modules:
  0.0 11.7 jit_solution(11701306065506921719)
XLA Ops:
  0.6 10.3 %shard_map.58 = (bf16[4,1,32,1024]{3,2,1,0:T(8,128)(2,1)S(1)}, f32[8,4,1,256]{3,2,1,0:T(1,128)S(1)}, f32[8,4,1,256]{3,2,1,0:T(1,128)S(1)}, f32[8,4,1,256]{3,2,1,0:T(1,128)S(1)}) custom-call(bf16[4,128,8,128]{3,2,1,0:T(8,128)(2,1)} %fields_hbm.1, s32[32,8,128]{2,1,0:T(8,128)} %bracket_hbm.1, bf16[32,8,128]{2,1,0:T(8,128)(2,1)} %fraction_hbm.1), custom_call_target="tpu_custom_call" | custom-call | tf_op jit(solution)/shard_map/pallas_call | solution.py:279
  10.9 0.8 %shard_map.59 = (bf16[4,1,32,1024]{3,2,1,0:T(8,128)(2,1)}, f32[4,1,32]{2,1,0:T(1,128)}, f32[4,1,32]{2,1,0:T(1,128)}) custom-call(bf16[4,1,32,1024]{3,2,1,0:T(8,128)(2,1)S(1)} %get-tuple-element.10.rows_vmem, f32[8,4,1,256]{3,2,1,0:T(1,128)S(1)} %get-tuple-element.11.sums, f32[8,4,1,256]{3,2,1,0:T(1,128)S(1)} %get-tuple-element.12.cross_lo, ...), custom_call_target="tpu_custom_call" | custom-call | tf_op jit(solution)/shard_map/pallas_call | solution.py:311
